TPU v7x, 512 devices: a whole 4x8x8 slice. The times are simulated.
512 devices in a mesh: dom: 64 (over x, y, core), mem: 8 (over z).
Axes of the slice: x: 4, y: 8, z: 8, core: 2. Of those that a mesh axis runs over, the one named last changes fastest.
Arguments:
- ensemble: bfloat16 [48, 32, 262144], P('mem', None, 'dom'), may hold values from -6 to 6
- observed: float32 [32, 65536], P(None, 'dom'), may hold values from -6 to 6
- tile_weight: bfloat16 [6144, 128, 128], P('dom')
- tile_block: int32 [6144], P('dom'), may hold values from 0 to 31
- tile_target: int32 [6144], P('dom'), may hold values from 0 to 511, as said below
- tile_count: int32 [64], P('dom'), may hold values from 48 to 96, as said below
Outputs:
- crps: float32 [32, 65536], P(None, 'dom')
Inputs may be any that keep to these rules, and one draw needn't show every extreme that they name: `tile_block`: a slot's source block, counted within its partition's cells. `tile_target`: slot k belongs to partition p = k // 96; its target tile is owned by one of the partitions p - 4 to p + 4, where partition o owns the 8 target tiles from o * 8 on. The live slots of partition p are the first tile_count[p] of its list; the rest are padding.
All inputs are finite; a program needn't handle non-finite values.
Results may differ from a plain program's by a relative error of at most 0.0003.
Values sent between devices are 32-bit elements; how exact they have to be, the bound alone decides.
No kernel may reach another device: no remote copies, remote signals or barrier semaphores. Data moves between devices by JAX's collectives and lax.ppermute only.
A program may use at most 64 MiB of HBM per device.

v0:
```python
import math
import jax
import jax.numpy as jnp
from jax import lax
from jax.sharding import PartitionSpec as P

REACH = 4


def from_behind(value, axis, steps):
    count = lax.axis_size(axis)
    first, last = (max(0, -steps), min(count, count - steps))
    return lax.ppermute(value, axis, [(source, source + steps) for source in range(first, last)])


def sent_to_all(shard, axis):
    copies = jnp.broadcast_to(shard, (lax.axis_size(axis), *shard.shape))
    return lax.all_to_all(copies, axis, split_axis=0, concat_axis=0, tiled=True)


def laid_out(pieces, dim):
    pieces = jnp.moveaxis(pieces, 0, dim)
    lengths = pieces.shape
    return pieces.reshape(*lengths[:dim], lengths[dim] * lengths[dim + 1], *lengths[dim + 2 :])


def gathered_copies(shard, axis, dim):
    pieces = sent_to_all(shard, axis)
    return laid_out(pieces, dim)


def pair_total(left_set, right_set):
    flat_left = left_set.reshape(left_set.shape[0], -1)
    flat_right = right_set.reshape(right_set.shape[0], -1)
    total_columns = flat_left.shape[1]
    block_span = math.gcd(total_columns, 1024)

    def block_pairs(first_column):
        left_cols = lax.dynamic_slice_in_dim(flat_left, first_column, block_span, 1)
        right_cols = lax.dynamic_slice_in_dim(flat_right, first_column, block_span, 1)
        return jnp.sum(jnp.abs(left_cols[:, None, :] - right_cols[None, :, :]), axis=(0, 1))

    column_starts = jnp.arange(total_columns // block_span, dtype=jnp.int32) * block_span
    return lax.map(block_pairs, column_starts).reshape(left_set.shape[1:])


def on_device(ensemble, observed, tile_weight, tile_block, tile_target, tile_count):
    groups, levels, src_cells = ensemble.shape
    block_cells = tile_weight.shape[1]
    channels = groups * levels
    tile_slots = tile_block.shape[0]
    values = ensemble.reshape(channels, src_cells // block_cells, block_cells)
    picked = jnp.take(values, tile_block, axis=1)
    partial_value = jnp.einsum(
        "csi,sij->scj", picked, tile_weight, preferred_element_type=jnp.float32
    )
    owned = observed.shape[1] // block_cells
    window = 2 * REACH + 1
    device = lax.axis_index("dom")
    local_tile = tile_target - (device - REACH) * owned
    rows_index = jnp.arange(window * owned, dtype=jnp.int32)
    is_live = jnp.arange(tile_slots, dtype=jnp.int32) < tile_count[0]
    chooser = ((rows_index[:, None] == local_tile[None, :]) & is_live[None, :]).astype(jnp.float32)
    owner_parts = jnp.dot(
        chooser,
        partial_value.reshape(tile_slots, channels * block_cells),
        precision=lax.Precision.HIGHEST,
        preferred_element_type=jnp.float32,
    )
    owner_parts = owner_parts.reshape(window, owned, channels * block_cells)
    summed = owner_parts[REACH]
    pending = {}
    for offset in range(1, REACH + 1):
        pending[1, offset] = owner_parts[REACH + offset]
        pending[-1, offset] = owner_parts[REACH - offset]
    for level_bit in range(REACH.bit_length()):
        stride = 1 << level_bit
        for heading in (1, -1):
            moving = [
                offset
                for offset in range(1, REACH + 1)
                if (heading, offset) in pending and offset & stride
            ]
            if moving:
                outgoing = jnp.stack([pending.pop((heading, offset)) for offset in moving])
                incoming = from_behind(outgoing, "dom", heading * stride)
                for position, offset in enumerate(moving):
                    landing = offset - stride
                    if landing == 0:
                        summed = summed + incoming[position]
                    else:
                        pending[heading, landing] = pending[heading, landing] + incoming[position]
    remapped = (
        summed.reshape(owned, groups, levels, block_cells)
        .transpose(1, 2, 0, 3)
        .reshape(groups, levels, owned * block_cells)
    )
    members = groups * lax.axis_size("mem")
    norm_pairs = 2.0 * members * (members - 1)
    regrouped = lax.all_to_all(remapped, "mem", split_axis=2, concat_axis=0, tiled=True)
    part_cells = regrouped.shape[2]
    observed_part = lax.dynamic_slice_in_dim(
        observed, lax.axis_index("mem") * part_cells, part_cells, 1
    )
    skill_sum = jnp.sum(jnp.abs(regrouped - observed_part[None]), axis=0)
    spread = pair_total(regrouped, regrouped)
    score_part = skill_sum / members - spread / norm_pairs
    return gathered_copies(score_part, "mem", 1)


def solution(mesh):
    return jax.shard_map(
        on_device,
        mesh=mesh,
        in_specs=(
            P("mem", None, "dom"),
            P(None, "dom"),
            P("dom", None, None),
            P("dom"),
            P("dom"),
            P("dom"),
        ),
        out_specs=P(None, "dom"),
        check_vma=False,
    )
```

profile of v0, /device:TPU:2, one launch (start us, length us, event | category | flops | bytes accessed | tf_op | source)
XLA Modules:
  0.0 198.6 jit_solution(17366331627590352062)
XLA Ops:
  1.6 1.7 copy.26
  3.4 1.8 copy.18
  5.9 4.8 %gather_fusion = bf16[96,192,128]{2,1,0:T(8,128)(2,1)} fusion(bf16[192,32,128]{2,0,1:T(8,128)(2,1)} %copy.18, s32[1024]{0:T(1024)S(1)} %pad_clamp_fusion), kind=kCustom, calls=%fused_computation | custom fusion | bytes 9437568 | tf_op jit(solution)/shard_map/jit(_take)/gather | solution.py:53
  10.7 3.4 %fusion.3 = f32[96,192,128]{2,1,0:T(8,128)S(1)} fusion(bf16[96,128,128]{2,1,0:T(8,128)(2,1)S(1)} %copy-done, bf16[96,192,128]{2,1,0:T(8,128)(2,1)} %gather_fusion, pred[96]{0:T(512)(128)(4,1)S(1)} %compare_and_fusion), kind=kOutput, calls=%fused_computation.6 | convolution fusion | flops 606339072 | bytes 17301600 | tf_op jit(solution)/shard_map/csi,sij->scj/dot_general | solution.py:54
  14.1 10.0 %fusion = f32[72,24576]{1,0:T(8,128)S(1)} fusion(f32[12,8,192,128]{3,2,1,0:T(8,128)S(1)} %bitcast.71, s32[96]{0:T(128)S(1)} %broadcast_subtract_fusion, pred[96]{0:T(512)(128)(4,1)S(1)} %iota_compare_fusion.1), kind=kOutput, calls=%fused_computation.3 | convolution fusion | flops 2038445568 | bytes 16515552 | tf_op jit(solution)/shard_map/dot_general | solution.py:64
  24.6 4.8 %collective-permute-start.1 = (f32[2,8,24576]{2,1,0:T(8,128)S(1)}, f32[2,8,24576]{2,1,0:T(8,128)S(1)}, u32[]{:S(2)}, u32[]{:S(2)}) collective-permute-start(f32[2,8,24576]{2,1,0:T(8,128)S(1)} %pad_maximum_fusion.1), channel_id=1, source_target_pairs={{8,0},{16,8},{24,16},{32,24},{40,32},{48,40},{56,48},{64,56},{72,6... | collective-permute-start | bytes 4718600 | tf_op jit(solution)/shard_map/ppermute | solution.py:13
  29.5 1.9 collective-permute-start
  31.4 2.1 %collective-permute-start.4 = (f32[1,8,24576]{2,1,0:T(8,128)S(1)}, f32[1,8,24576]{2,1,0:T(8,128)S(1)}, u32[]{:S(2)}, u32[]{:S(2)}) collective-permute-start(f32[1,8,24576]{2,1,0:T(8,128)S(1)} %get-tuple-element.52), channel_id=1, source_target_pairs={{0,32},{8,40},{16,48},{24,56},{32,64},{40,72},{48,80},{56,88},{64,... | collective-permute-start | bytes 2359304 | tf_op jit(solution)/shard_map/ppermute | solution.py:13
  33.6 6.9 %collective-permute-start.5 = (f32[1,8,24576]{2,1,0:T(8,128)S(1)}, f32[1,8,24576]{2,1,0:T(8,128)S(1)}, u32[]{:S(2)}, u32[]{:S(2)}) collective-permute-start(f32[1,8,24576]{2,1,0:T(8,128)S(1)} %get-tuple-element.51), channel_id=1, source_target_pairs={{32,0},{40,8},{48,16},{56,24},{64,32},{72,40},{80,48},{88,56},{96,... | collective-permute-start | bytes 2359304 | tf_op jit(solution)/shard_map/ppermute | solution.py:13
  40.5 28.0 %collective-permute-done.1 = f32[2,8,24576]{2,1,0:T(8,128)S(1)} collective-permute-done((f32[2,8,24576]{2,1,0:T(8,128)S(1)}, f32[2,8,24576]{2,1,0:T(8,128)S(1)}, u32[]{:S(2)}, u32[]{:S(2)}) %collective-permute-start.1) | collective-permute-done | bytes 1572896 | tf_op jit(solution)/shard_map/ppermute | solution.py:13
  68.5 3.9 %collective-permute-done = f32[2,8,24576]{2,1,0:T(8,128)S(1)} collective-permute-done((f32[2,8,24576]{2,1,0:T(8,128)S(1)}, f32[2,8,24576]{2,1,0:T(8,128)S(1)}, u32[]{:S(2)}, u32[]{:S(2)}) %collective-permute-start) | collective-permute-done | bytes 1572896 | tf_op jit(solution)/shard_map/ppermute | solution.py:13
  72.6 1.9 collective-permute-start.2
  74.6 6.0 %collective-permute-start.3 = (f32[1,8,24576]{2,1,0:T(8,128)S(1)}, f32[1,8,24576]{2,1,0:T(8,128)S(1)}, u32[]{:S(2)}, u32[]{:S(2)}) collective-permute-start(f32[1,8,24576]{2,1,0:T(8,128)S(1)} %get-tuple-element.58), channel_id=1, source_target_pairs={{16,0},{24,8},{32,16},{40,24},{48,32},{56,40},{64,48},{72,56},{80,... | collective-permute-start | bytes 2359304 | tf_op jit(solution)/shard_map/ppermute | solution.py:13
  80.6 1.7 collective-permute-done.5
  82.4 18.5 %collective-permute-done.2 = f32[1,8,24576]{2,1,0:T(8,128)S(1)} collective-permute-done((f32[1,8,24576]{2,1,0:T(8,128)S(1)}, f32[1,8,24576]{2,1,0:T(8,128)S(1)}, u32[]{:S(2)}, u32[]{:S(2)}) %collective-permute-start.2) | collective-permute-done | bytes 786464 | tf_op jit(solution)/shard_map/ppermute | solution.py:13
  100.9 1.2 add_bitcast_fusion
  102.1 4.2 %copy.19 = f32[6,32,8,128]{1,0,3,2:T(8,128)} copy(f32[6,32,8,128]{3,2,1,0:T(8,128)} %add_bitcast_fusion) | data formatting | bytes 1572864 | tf_op jit(solution)/shard_map/transpose | solution.py:95
  106.3 4.6 %reshape.70 = f32[8,1,24576]{2,1,0:T(1,128)} reshape(f32[1024,6,32]{2,1,0:T(8,128)} %bitcast.74) | data formatting | bytes 1572864
  110.9 12.8 %all-to-all-start = ((f32[8,1,24576]{2,1,0:T(1,128)}), f32[8,1,24576]{2,1,0:T(1,128)}, u32[]{:S(2)}, u32[]{:S(2)}) async-start(f32[8,1,24576]{2,1,0:T(1,128)} %reshape.70), calls=%async_computation | async-start | bytes 1572864 | tf_op jit(solution)/shard_map/all_to_all | solution.py:100
  124.4 23.2 %all-to-all-done = f32[8,1,24576]{2,1,0:T(1,128)} async-done(((f32[8,1,24576]{2,1,0:T(1,128)}), f32[8,1,24576]{2,1,0:T(1,128)}, u32[]{:S(2)}, u32[]{:S(2)}) %all-to-all-start) | async-done | bytes 786464 | tf_op jit(solution)/shard_map/all_to_all | solution.py:100
  148.1 4.5 %reduce.1 = f32[8,24576]{1,0:T(8,128)} reduce(f32[8,1,24576]{2,1,0:T(1,128)} %all-to-all-done, f32[]{:T(128)} %broadcast.36), dimensions={1}, to_apply=%all_to_all.14.reduce_sub_computation | reduce | bytes 1572868 | tf_op jit(solution)/shard_map/all_to_all | solution.py:100
  152.6 4.5 %reshape.71 = f32[1024,6,32]{2,1,0:T(8,128)} reshape(f32[8,24576]{1,0:T(8,128)} %reduce.1) | data formatting | bytes 1572864
  157.1 3.4 %copy.21 = f32[8,6,32,128]{3,2,1,0:T(8,128)} copy(f32[8,6,32,128]{2,1,3,0:T(8,128)} %bitcast.72) | data formatting | bytes 1572864 | tf_op jit(solution)/shard_map/all_to_all | solution.py:100
  160.6 2.5 %copy.35 = f32[6,8,32,128]{3,1,2,0:T(8,128)} copy(f32[6,8,32,128]{3,2,1,0:T(8,128)} %bitcast.77) | data formatting | bytes 1572864
  163.0 17.7 %while.11 = (s32[]{:T(128)}, f32[4,1024]{1,0:T(4,128)S(1)}, s32[4]{0:T(128)S(1)}, f32[48,4096]{1,0:T(8,128)}, s32[]{:T(128)}, /*index=5*/s32[]{:T(128)}, s32[]{:T(128)}) while((s32[]{:T(128)}, f32[4,1024]{1,0:T(4,128)S(1)}, s32[4]{0:T(128)S(1)}, f32[48,4096]{1,0:T(8,128)}, s32[]{:T(128)}, /*index=5*/s32[]{:T(128)}, s32[]{:T(128)}) %tuple.33), condition=%wide.region_3.4_spmd, body=%wide.region_1.3_spmd.sunk | while | flops 7076869 | bytes 602243 | solution.py:44
  166.3 1.1 abs_reduce_fusion.2
  170.7 1.1 abs_reduce_fusion.2
  175.1 1.1 abs_reduce_fusion.2
  179.6 1.1 abs_reduce_fusion.2
  180.7 3.9 %copy.23 = f32[6,32,8,128]{3,2,1,0:T(8,128)} copy(f32[6,32,8,128]{1,0,3,2:T(8,128)} %bitcast.73) | data formatting | bytes 1572864 | tf_op jit(solution)/shard_map/all_to_all | solution.py:100
  184.7 1.2 fusion.9
  186.0 11.9 %all_to_all.20 = f32[8,32,128]{2,1,0:T(8,128)S(1)} all-to-all(f32[8,32,128]{2,1,0:T(8,128)S(1)} %broadcast_in_dim.35), channel_id=1, replica_groups=mesh['dom'=64,'mem'=8] {'mem'}, dimensions={0} | all-to-all | bytes 262144 | tf_op jit(solution)/shard_map/all_to_all | solution.py:18
  (36 shorter events, 11.2 us)
Async XLA Ops:
  0.0 10.7 %copy-start = (bf16[96,128,128]{2,1,0:T(8,128)(2,1)S(1)}, bf16[96,128,128]{2,1,0:T(8,128)(2,1)}, u32[]{:S(2)}) copy-start(bf16[96,128,128]{2,1,0:T(8,128)(2,1)} %param.10) | copy-start | bytes 9437188
  0.0 5.8 %copy-start.1 = (s32[96]{0:T(128)S(1)}, s32[96]{0:T(128)}, u32[]{:S(2)}) copy-start(s32[96]{0:T(128)} %param.12) | copy-start | bytes 1156
  24.6 43.9 %collective-permute-start.1 = (f32[2,8,24576]{2,1,0:T(8,128)S(1)}, f32[2,8,24576]{2,1,0:T(8,128)S(1)}, u32[]{:S(2)}, u32[]{:S(2)}) collective-permute-start(f32[2,8,24576]{2,1,0:T(8,128)S(1)} %pad_maximum_fusion.1), channel_id=1, source_target_pairs={{8,0},{16,8},{24,16},{32,24},{40,32},{48,40},{56,48},{64,56},{72,6... | collective-permute-start | bytes 4718600 | tf_op jit(solution)/shard_map/ppermute | solution.py:13
  29.5 42.9 %collective-permute-start = (f32[2,8,24576]{2,1,0:T(8,128)S(1)}, f32[2,8,24576]{2,1,0:T(8,128)S(1)}, u32[]{:S(2)}, u32[]{:S(2)}) collective-permute-start(f32[2,8,24576]{2,1,0:T(8,128)S(1)} %pad_maximum_fusion), channel_id=1, source_target_pairs={{0,8},{8,16},{16,24},{24,32},{32,40},{40,48},{48,56},{56,64},{64,7... | collective-permute-start | bytes 4718600 | tf_op jit(solution)/shard_map/ppermute | solution.py:13
  31.4 49.2 %collective-permute-start.4 = (f32[1,8,24576]{2,1,0:T(8,128)S(1)}, f32[1,8,24576]{2,1,0:T(8,128)S(1)}, u32[]{:S(2)}, u32[]{:S(2)}) collective-permute-start(f32[1,8,24576]{2,1,0:T(8,128)S(1)} %get-tuple-element.52), channel_id=1, source_target_pairs={{0,32},{8,40},{16,48},{24,56},{32,64},{40,72},{48,80},{56,88},{64,... | collective-permute-start | bytes 2359304 | tf_op jit(solution)/shard_map/ppermute | solution.py:13
  33.6 48.8 %collective-permute-start.5 = (f32[1,8,24576]{2,1,0:T(8,128)S(1)}, f32[1,8,24576]{2,1,0:T(8,128)S(1)}, u32[]{:S(2)}, u32[]{:S(2)}) collective-permute-start(f32[1,8,24576]{2,1,0:T(8,128)S(1)} %get-tuple-element.51), channel_id=1, source_target_pairs={{32,0},{40,8},{48,16},{56,24},{64,32},{72,40},{80,48},{88,56},{96,... | collective-permute-start | bytes 2359304 | tf_op jit(solution)/shard_map/ppermute | solution.py:13
  72.6 28.2 %collective-permute-start.2 = (f32[1,8,24576]{2,1,0:T(8,128)S(1)}, f32[1,8,24576]{2,1,0:T(8,128)S(1)}, u32[]{:S(2)}, u32[]{:S(2)}) collective-permute-start(f32[1,8,24576]{2,1,0:T(8,128)S(1)} %get-tuple-element.57), channel_id=1, source_target_pairs={{0,16},{8,24},{16,32},{24,40},{32,48},{40,56},{48,64},{56,72},{64,... | collective-permute-start | bytes 2359304 | tf_op jit(solution)/shard_map/ppermute | solution.py:13
  74.6 26.3 %collective-permute-start.3 = (f32[1,8,24576]{2,1,0:T(8,128)S(1)}, f32[1,8,24576]{2,1,0:T(8,128)S(1)}, u32[]{:S(2)}, u32[]{:S(2)}) collective-permute-start(f32[1,8,24576]{2,1,0:T(8,128)S(1)} %get-tuple-element.58), channel_id=1, source_target_pairs={{16,0},{24,8},{32,16},{40,24},{48,32},{56,40},{64,48},{72,56},{80,... | collective-permute-start | bytes 2359304 | tf_op jit(solution)/shard_map/ppermute | solution.py:13
  110.9 36.7 %all-to-all-start = ((f32[8,1,24576]{2,1,0:T(1,128)}), f32[8,1,24576]{2,1,0:T(1,128)}, u32[]{:S(2)}, u32[]{:S(2)}) async-start(f32[8,1,24576]{2,1,0:T(1,128)} %reshape.70), calls=%async_computation | async-start | bytes 1572864 | tf_op jit(solution)/shard_map/all_to_all | solution.py:100
where the time goes:
time: 200 us; the launch traced here: 199 us
  waiting for transfers between devices  75.3 us (38%)
  local copies, waits for them, and re-layouts  40.5 us (20%)
  starting transfers between devices  36.5 us (18%)
  other arithmetic  13.4 us (7%)
  matrix products  13.4 us (7%)
  blocking collectives  11.9 us (6%)
  loops' own time  6.69 us (3%)
    ppermute x6, waiting for transfers between devices, from_behind(): lax.ppermute(value, axis, [(source, source + steps) for source in range(f...  52.1 us
    ppermute x6, starting transfers between devices, from_behind(): lax.ppermute(value, axis, [(source, source + steps) for source in range(f...  23.7 us
    all_to_all x1, waiting for transfers between devices, on_device(): lax.all_to_all(remapped, 'mem', split_axis=2, concat_axis=0, tiled=True)  23.2 us
    unnamed x8, local copies, waits for them, and re-layouts  13.3 us
    all_to_all x1, starting transfers between devices, on_device(): lax.all_to_all(remapped, 'mem', split_axis=2, concat_axis=0, tiled=True)  12.8 us
    all_to_all x1, blocking collectives, sent_to_all(): return lax.all_to_all(copies, axis, split_axis=0, concat_axis=0, tiled=True)  11.9 us
    dot_general x1, matrix products, on_device(): jnp.dot(chooser, partial_value.reshape(tile_slots, channels * block_cells...  10 us
    all_to_all x3, local copies, waits for them, and re-layouts, on_device(): lax.all_to_all(remapped, 'mem', split_axis=2, concat_axis=0, tiled=True)  7.94 us
  transfers between devices with their start and end apart: 7, of which 5 were waited for; matrix products, arithmetic and copies ran while one was open for 1% of the time, Pallas kernels for 0%

commit v1 on v0

--- a/solution.py
+++ b/solution.py
@@ -97,7 +97,10 @@
     )
     members = groups * lax.axis_size("mem")
     norm_pairs = 2.0 * members * (members - 1)
-    regrouped = lax.all_to_all(remapped, "mem", split_axis=2, concat_axis=0, tiled=True)
+    regrouped = jnp.concatenate(
+        lax.all_to_all(jnp.stack(jnp.split(remapped, lax.axis_size("mem"), axis=2)), "mem", 0, 0),
+        axis=0,
+    )
     part_cells = regrouped.shape[2]
     observed_part = lax.dynamic_slice_in_dim(
         observed, lax.axis_index("mem") * part_cells, part_cells, 1

time: 200 us -> 190 us (0.950)
  local copies, waits for them, and re-layouts: 40.5 us -> 34 us
  other arithmetic: 13.4 us -> 8.91 us
    all_to_all x3 -> x0, local copies, waits for them, and re-layouts: 7.94 us -> none  [on_device(): lax.all_to_all(remapped, 'mem', split_axis=2, concat_axis=0, tiled=True)]
    all_to_all x1 -> x0, other arithmetic: 4.51 us -> none  [on_device(): lax.all_to_all(remapped, 'mem', split_axis=2, concat_axis=0, tiled=True)]
    transpose x1 -> x0, local copies, waits for them, and re-layouts: 4.22 us -> none  [on_device(): remapped = summed.reshape(owned, groups, levels, block_cells).transpose(1...]
    reshape x0 -> x1, local copies, waits for them, and re-layouts: none -> 2.13 us  [on_device(): remapped = summed.reshape(owned, groups, levels, block_cells).transpose(1...]
    unnamed x8 -> x13, local copies, waits for them, and re-layouts: 13.3 us -> 15 us
where the time goes in v1:
time: 190 us; the launch traced here: 189 us
  waiting for transfers between devices  75.3 us (40%)
  starting transfers between devices  36.5 us (19%)
  local copies, waits for them, and re-layouts  34 us (18%)
  matrix products  13.4 us (7%)
  blocking collectives  11.9 us (6%)
  other arithmetic  8.91 us (5%)
  loops' own time  7.75 us (4%)
    ppermute x6, waiting for transfers between devices, from_behind(): lax.ppermute(value, axis, [(source, source + steps) for source in range(f...  52.1 us
    ppermute x6, starting transfers between devices, from_behind(): lax.ppermute(value, axis, [(source, source + steps) for source in range(f...  23.7 us
    all_to_all x1, waiting for transfers between devices, on_device(): lax.all_to_all(jnp.stack(jnp.split(remapped, lax.axis_size('mem'), axis=2...  23.2 us
    unnamed x13, local copies, waits for them, and re-layouts  15 us
    all_to_all x1, starting transfers between devices, on_device(): lax.all_to_all(jnp.stack(jnp.split(remapped, lax.axis_size('mem'), axis=2...  12.8 us
    all_to_all x1, blocking collectives, sent_to_all(): return lax.all_to_all(copies, axis, split_axis=0, concat_axis=0, tiled=True)  11.9 us
    dot_general x1, matrix products, on_device(): jnp.dot(chooser, partial_value.reshape(tile_slots, channels * block_cells...  10 us
    another operation x1, loops' own time, pair_total(): return lax.map(block_pairs, column_starts).reshape(left_set.shape[1:])  7.75 us
  transfers between devices with their start and end apart: 7, of which 5 were waited for; matrix products, arithmetic and copies ran while one was open for 1% of the time, Pallas kernels for 0%

profile of v1, /device:TPU:2, one launch (start us, length us, event | category | flops | bytes accessed | tf_op | source)
XLA Modules:
  0.0 188.6 jit_solution(16534641953892245516)
XLA Ops:
  1.6 1.7 copy.14
  3.4 1.8 copy.11
  5.9 4.9 %gather_fusion = bf16[96,192,128]{2,1,0:T(8,128)(2,1)} fusion(bf16[192,32,128]{2,0,1:T(8,128)(2,1)} %copy.11, s32[1024]{0:T(1024)S(1)} %pad_clamp_fusion), kind=kCustom, calls=%fused_computation | custom fusion | bytes 9437568 | tf_op jit(solution)/shard_map/jit(_take)/gather | solution.py:53
  10.7 3.4 %fusion.3 = f32[96,192,128]{2,1,0:T(8,128)S(1)} fusion(bf16[96,128,128]{2,1,0:T(8,128)(2,1)S(1)} %copy-done, bf16[96,192,128]{2,1,0:T(8,128)(2,1)} %gather_fusion, pred[96]{0:T(512)(128)(4,1)S(1)} %compare_and_fusion), kind=kOutput, calls=%fused_computation.6 | convolution fusion | flops 606339072 | bytes 17301600 | tf_op jit(solution)/shard_map/csi,sij->scj/dot_general | solution.py:54
  14.1 10.0 %fusion = f32[72,24576]{1,0:T(8,128)S(1)} fusion(f32[12,8,192,128]{3,2,1,0:T(8,128)S(1)} %bitcast.93, s32[96]{0:T(128)S(1)} %broadcast_subtract_fusion, pred[96]{0:T(512)(128)(4,1)S(1)} %iota_compare_fusion.1), kind=kOutput, calls=%fused_computation.3 | convolution fusion | flops 2038445568 | bytes 16515552 | tf_op jit(solution)/shard_map/dot_general | solution.py:64
  24.6 4.8 %collective-permute-start.1 = (f32[2,8,24576]{2,1,0:T(8,128)S(1)}, f32[2,8,24576]{2,1,0:T(8,128)S(1)}, u32[]{:S(2)}, u32[]{:S(2)}) collective-permute-start(f32[2,8,24576]{2,1,0:T(8,128)S(1)} %pad_maximum_fusion.1), channel_id=1, source_target_pairs={{8,0},{16,8},{24,16},{32,24},{40,32},{48,40},{56,48},{64,56},{72,6... | collective-permute-start | bytes 4718600 | tf_op jit(solution)/shard_map/ppermute | solution.py:13
  29.5 1.9 %collective-permute-start = (f32[2,8,24576]{2,1,0:T(8,128)S(1)}, f32[2,8,24576]{2,1,0:T(8,128)S(1)}, u32[]{:S(2)}, u32[]{:S(2)}) collective-permute-start(f32[2,8,24576]{2,1,0:T(8,128)S(1)} %pad_maximum_fusion), channel_id=1, source_target_pairs={{0,8},{8,16},{16,24},{24,32},{32,40},{40,48},{48,56},{56,64},{64,7... | collective-permute-start | bytes 4718600 | tf_op jit(solution)/shard_map/ppermute | solution.py:13
  31.5 2.1 %collective-permute-start.4 = (f32[1,8,24576]{2,1,0:T(8,128)S(1)}, f32[1,8,24576]{2,1,0:T(8,128)S(1)}, u32[]{:S(2)}, u32[]{:S(2)}) collective-permute-start(f32[1,8,24576]{2,1,0:T(8,128)S(1)} %get-tuple-element.52), channel_id=1, source_target_pairs={{0,32},{8,40},{16,48},{24,56},{32,64},{40,72},{48,80},{56,88},{64,... | collective-permute-start | bytes 2359304 | tf_op jit(solution)/shard_map/ppermute | solution.py:13
  33.6 6.9 %collective-permute-start.5 = (f32[1,8,24576]{2,1,0:T(8,128)S(1)}, f32[1,8,24576]{2,1,0:T(8,128)S(1)}, u32[]{:S(2)}, u32[]{:S(2)}) collective-permute-start(f32[1,8,24576]{2,1,0:T(8,128)S(1)} %get-tuple-element.51), channel_id=1, source_target_pairs={{32,0},{40,8},{48,16},{56,24},{64,32},{72,40},{80,48},{88,56},{96,... | collective-permute-start | bytes 2359304 | tf_op jit(solution)/shard_map/ppermute | solution.py:13
  40.5 28.0 %collective-permute-done.1 = f32[2,8,24576]{2,1,0:T(8,128)S(1)} collective-permute-done((f32[2,8,24576]{2,1,0:T(8,128)S(1)}, f32[2,8,24576]{2,1,0:T(8,128)S(1)}, u32[]{:S(2)}, u32[]{:S(2)}) %collective-permute-start.1) | collective-permute-done | bytes 1572896 | tf_op jit(solution)/shard_map/ppermute | solution.py:13
  68.5 3.9 %collective-permute-done = f32[2,8,24576]{2,1,0:T(8,128)S(1)} collective-permute-done((f32[2,8,24576]{2,1,0:T(8,128)S(1)}, f32[2,8,24576]{2,1,0:T(8,128)S(1)}, u32[]{:S(2)}, u32[]{:S(2)}) %collective-permute-start) | collective-permute-done | bytes 1572896 | tf_op jit(solution)/shard_map/ppermute | solution.py:13
  72.7 1.9 %collective-permute-start.2 = (f32[1,8,24576]{2,1,0:T(8,128)S(1)}, f32[1,8,24576]{2,1,0:T(8,128)S(1)}, u32[]{:S(2)}, u32[]{:S(2)}) collective-permute-start(f32[1,8,24576]{2,1,0:T(8,128)S(1)} %get-tuple-element.57), channel_id=1, source_target_pairs={{0,16},{8,24},{16,32},{24,40},{32,48},{40,56},{48,64},{56,72},{64,... | collective-permute-start | bytes 2359304 | tf_op jit(solution)/shard_map/ppermute | solution.py:13
  74.6 6.0 %collective-permute-start.3 = (f32[1,8,24576]{2,1,0:T(8,128)S(1)}, f32[1,8,24576]{2,1,0:T(8,128)S(1)}, u32[]{:S(2)}, u32[]{:S(2)}) collective-permute-start(f32[1,8,24576]{2,1,0:T(8,128)S(1)} %get-tuple-element.58), channel_id=1, source_target_pairs={{16,0},{24,8},{32,16},{40,24},{48,32},{56,40},{64,48},{72,56},{80,... | collective-permute-start | bytes 2359304 | tf_op jit(solution)/shard_map/ppermute | solution.py:13
  80.6 1.7 collective-permute-done.5
  82.4 18.5 %collective-permute-done.2 = f32[1,8,24576]{2,1,0:T(8,128)S(1)} collective-permute-done((f32[1,8,24576]{2,1,0:T(8,128)S(1)}, f32[1,8,24576]{2,1,0:T(8,128)S(1)}, u32[]{:S(2)}, u32[]{:S(2)}) %collective-permute-start.2) | collective-permute-done | bytes 786464 | tf_op jit(solution)/shard_map/ppermute | solution.py:13
  100.9 1.2 add_bitcast_fusion
  102.1 2.1 %reshape.54 = f32[6,32,1024]{2,1,0:T(8,128)} reshape(f32[6,32,8,128]{3,2,1,0:T(8,128)} %add_bitcast_fusion) | data formatting | bytes 1572864 | tf_op jit(solution)/shard_map/reshape | solution.py:96
  104.3 1.5 fusion.15
  105.8 1.5 fusion.14
  107.3 1.5 fusion.13
  108.9 1.5 fusion.12
  110.4 1.5 fusion.11
  111.9 1.5 fusion.10
  113.5 1.5 fusion.9
  115.0 1.5 fusion.8
  116.5 12.8 %all-to-all-start = ((f32[8,6,32,128]{3,2,1,0:T(8,128)}), f32[8,6,32,128]{3,2,1,0:T(8,128)}, u32[]{:S(2)}, u32[]{:S(2)}) async-start(f32[8,6,32,128]{3,2,1,0:T(8,128)} %fusion.8), calls=%async_computation | async-start | bytes 1572864 | tf_op jit(solution)/shard_map/all_to_all | solution.py:101
  130.0 23.2 %all-to-all-done = f32[8,6,32,128]{3,2,1,0:T(8,128)} async-done(((f32[8,6,32,128]{3,2,1,0:T(8,128)}), f32[8,6,32,128]{3,2,1,0:T(8,128)}, u32[]{:S(2)}, u32[]{:S(2)}) %all-to-all-start) | async-done | bytes 786464 | tf_op jit(solution)/shard_map/all_to_all | solution.py:101
  153.2 2.5 %copy.23 = f32[6,8,32,128]{3,1,2,0:T(8,128)} copy(f32[6,8,32,128]{3,2,1,0:T(8,128)} %bitcast.38) | data formatting | bytes 1572864
  155.7 19.0 %while.11 = (s32[]{:T(128)}, f32[4,1024]{1,0:T(4,128)S(1)}, s32[4]{0:T(128)S(1)}, f32[48,4096]{1,0:T(8,128)}, s32[]{:T(128)}, /*index=5*/s32[]{:T(128)}, s32[]{:T(128)}) while((s32[]{:T(128)}, f32[4,1024]{1,0:T(4,128)S(1)}, s32[4]{0:T(128)S(1)}, f32[48,4096]{1,0:T(8,128)}, s32[]{:T(128)}, /*index=5*/s32[]{:T(128)}, s32[]{:T(128)}) %tuple.33), condition=%wide.region_3.4_spmd, body=%wide.region_1.3_spmd.sunk | while | flops 7076869 | bytes 602243 | solution.py:44
  159.3 1.1 abs_reduce_fusion.3
  174.7 1.2 abs_reduce_fusion.1
  176.0 11.9 %all_to_all.10 = f32[8,32,128]{2,1,0:T(8,128)S(1)} all-to-all(f32[8,32,128]{2,1,0:T(8,128)S(1)} %broadcast_in_dim.35), channel_id=1, replica_groups=mesh['dom'=64,'mem'=8] {'mem'}, dimensions={0} | all-to-all | bytes 262144 | tf_op jit(solution)/shard_map/all_to_all | solution.py:18
  (38 shorter events, 14.1 us)
Async XLA Ops:
  0.0 10.7 %copy-start = (bf16[96,128,128]{2,1,0:T(8,128)(2,1)S(1)}, bf16[96,128,128]{2,1,0:T(8,128)(2,1)}, u32[]{:S(2)}) copy-start(bf16[96,128,128]{2,1,0:T(8,128)(2,1)} %param.10) | copy-start | bytes 9437188
  0.0 5.8 %copy-start.1 = (s32[96]{0:T(128)S(1)}, s32[96]{0:T(128)}, u32[]{:S(2)}) copy-start(s32[96]{0:T(128)} %param.12) | copy-start | bytes 1156
  24.6 43.9 %collective-permute-start.1 = (f32[2,8,24576]{2,1,0:T(8,128)S(1)}, f32[2,8,24576]{2,1,0:T(8,128)S(1)}, u32[]{:S(2)}, u32[]{:S(2)}) collective-permute-start(f32[2,8,24576]{2,1,0:T(8,128)S(1)} %pad_maximum_fusion.1), channel_id=1, source_target_pairs={{8,0},{16,8},{24,16},{32,24},{40,32},{48,40},{56,48},{64,56},{72,6... | collective-permute-start | bytes 4718600 | tf_op jit(solution)/shard_map/ppermute | solution.py:13
  29.5 42.9 %collective-permute-start = (f32[2,8,24576]{2,1,0:T(8,128)S(1)}, f32[2,8,24576]{2,1,0:T(8,128)S(1)}, u32[]{:S(2)}, u32[]{:S(2)}) collective-permute-start(f32[2,8,24576]{2,1,0:T(8,128)S(1)} %pad_maximum_fusion), channel_id=1, source_target_pairs={{0,8},{8,16},{16,24},{24,32},{32,40},{40,48},{48,56},{56,64},{64,7... | collective-permute-start | bytes 4718600 | tf_op jit(solution)/shard_map/ppermute | solution.py:13
  31.5 49.2 %collective-permute-start.4 = (f32[1,8,24576]{2,1,0:T(8,128)S(1)}, f32[1,8,24576]{2,1,0:T(8,128)S(1)}, u32[]{:S(2)}, u32[]{:S(2)}) collective-permute-start(f32[1,8,24576]{2,1,0:T(8,128)S(1)} %get-tuple-element.52), channel_id=1, source_target_pairs={{0,32},{8,40},{16,48},{24,56},{32,64},{40,72},{48,80},{56,88},{64,... | collective-permute-start | bytes 2359304 | tf_op jit(solution)/shard_map/ppermute | solution.py:13
  33.6 48.8 %collective-permute-start.5 = (f32[1,8,24576]{2,1,0:T(8,128)S(1)}, f32[1,8,24576]{2,1,0:T(8,128)S(1)}, u32[]{:S(2)}, u32[]{:S(2)}) collective-permute-start(f32[1,8,24576]{2,1,0:T(8,128)S(1)} %get-tuple-element.51), channel_id=1, source_target_pairs={{32,0},{40,8},{48,16},{56,24},{64,32},{72,40},{80,48},{88,56},{96,... | collective-permute-start | bytes 2359304 | tf_op jit(solution)/shard_map/ppermute | solution.py:13
  72.7 28.2 %collective-permute-start.2 = (f32[1,8,24576]{2,1,0:T(8,128)S(1)}, f32[1,8,24576]{2,1,0:T(8,128)S(1)}, u32[]{:S(2)}, u32[]{:S(2)}) collective-permute-start(f32[1,8,24576]{2,1,0:T(8,128)S(1)} %get-tuple-element.57), channel_id=1, source_target_pairs={{0,16},{8,24},{16,32},{24,40},{32,48},{40,56},{48,64},{56,72},{64,... | collective-permute-start | bytes 2359304 | tf_op jit(solution)/shard_map/ppermute | solution.py:13
  74.6 26.3 %collective-permute-start.3 = (f32[1,8,24576]{2,1,0:T(8,128)S(1)}, f32[1,8,24576]{2,1,0:T(8,128)S(1)}, u32[]{:S(2)}, u32[]{:S(2)}) collective-permute-start(f32[1,8,24576]{2,1,0:T(8,128)S(1)} %get-tuple-element.58), channel_id=1, source_target_pairs={{16,0},{24,8},{32,16},{40,24},{48,32},{56,40},{64,48},{72,56},{80,... | collective-permute-start | bytes 2359304 | tf_op jit(solution)/shard_map/ppermute | solution.py:13
  116.5 36.7 %all-to-all-start = ((f32[8,6,32,128]{3,2,1,0:T(8,128)}), f32[8,6,32,128]{3,2,1,0:T(8,128)}, u32[]{:S(2)}, u32[]{:S(2)}) async-start(f32[8,6,32,128]{3,2,1,0:T(8,128)} %fusion.8), calls=%async_computation | async-start | bytes 1572864 | tf_op jit(solution)/shard_map/all_to_all | solution.py:101
